TPU v7x, 32 devices: a whole 2x2x4 slice. The times are simulated.
32 devices in a mesh: ctx: 16 (over z, y, x), tp: 2 (over core).
Axes of the slice: x: 2, y: 2, z: 4, core: 2. Of those that a mesh axis runs over, the one named last changes fastest.
Arguments:
- queries: bfloat16 [1024, 2560], P('ctx', 'tp'), may hold values from -100 to 100
- projected_keys: bfloat16 [1024, 512], P('ctx', 'tp'), may hold values from -30 to 30
- projected_values: bfloat16 [1024, 512], P('ctx', 'tp'), may hold values from -6 to 6
- hidden: bfloat16 [1024, 5120], P('ctx', 'tp'), may hold values from -6 to 6
- route_ids: int32 [1024, 1], P('ctx'), may hold values from 0 to 15; in each aligned block of 64 rows (0 to 63, 64 to 127, ...) at most 6 rows name the same one
- route_gain: float32 [1024], P('ctx'), may hold values from 0.25 to 1
- w_gate: bfloat16 [16, 5120, 4096], P('ctx', None, 'tp'), may hold values from -0.078125 to 0.078125
- w_up: bfloat16 [16, 5120, 4096], P('ctx', None, 'tp'), may hold values from -0.078125 to 0.078125
- w_down: bfloat16 [16, 4096, 5120], P('ctx', None, 'tp'), may hold values from -0.09375 to 0.09375
Outputs:
- attended: bfloat16 [1024, 2560], P('ctx', 'tp')
- mixed: bfloat16 [1024, 5120], P('ctx', 'tp')
Inputs may be any that keep to these rules, and one draw needn't show every extreme that they name: `route_ids`: within the rows of one device (aligned blocks of 64 rows) no expert is named more than 6 times, a bound that some block reaches.
All inputs are finite; a program needn't handle non-finite values.
Results may differ from a plain program's by a relative error of at most 0.0057.
Values may be sent and summed in bfloat16 or wider, within the bound.
No kernel may reach another device: no remote copies, remote signals or barrier semaphores. Data moves between devices by JAX's collectives and lax.ppermute only.
A program may use at most 128 MiB of HBM per device.

v0:
```python
import math
import jax
import jax.numpy as jnp
from jax import lax
from jax.sharding import PartitionSpec as P

HEAD_SIZE = 128
EXPERTS = 16
CAP = 6
masked_score = -1e30


def body(
    queries, projected_keys, projected_values, hidden, route_ids, route_gain, w_gate, w_up, w_down
):
    tok_rows = queries.shape[0]
    width_q = queries.shape[1]
    width_kv = projected_keys.shape[1]
    ctx_count = lax.axis_size("ctx")
    ctx_index = lax.axis_index("ctx")
    offsets = jnp.arange(tok_rows, dtype=jnp.int32)
    query_use, key_use, value_use = (queries, projected_keys, projected_values)

    def position(device, offset):
        return device * tok_rows + offset

    query_pos = position(ctx_index, offsets)
    query_top = jnp.max(query_pos)
    kv_heads = width_kv // HEAD_SIZE
    head_group = width_q // HEAD_SIZE // kv_heads
    query_tensor = query_use.reshape(tok_rows, kv_heads, head_group, HEAD_SIZE)
    score_scale = HEAD_SIZE ** (-0.5)
    key_whole, value_whole = (
        lax.all_gather(key_use, "ctx", axis=0, tiled=True),
        lax.all_gather(value_use, "ctx", axis=0, tiled=True),
    )
    total_rows = key_whole.shape[0]
    block_rows = math.gcd(total_rows, 1024)

    def absorb_block(block_index, state):
        block_start = block_index * block_rows
        key_block = lax.dynamic_slice_in_dim(key_whole, block_start, block_rows, 0).reshape(
            block_rows, kv_heads, HEAD_SIZE
        )
        value_block = lax.dynamic_slice_in_dim(value_whole, block_start, block_rows, 0).reshape(
            block_rows, kv_heads, HEAD_SIZE
        )
        global_rows = block_start + jnp.arange(block_rows, dtype=jnp.int32)
        key_pos = position(global_rows // tok_rows, global_rows % tok_rows)

        def update(inner_state):
            running_max, running_sum, running_out = inner_state
            scores = (
                jnp.einsum(
                    "qhgd,khd->hgqk", query_tensor, key_block, preferred_element_type=jnp.float32
                )
                * score_scale
            )
            allowed = query_pos[:, None] >= key_pos[None, :]
            scores = jnp.where(allowed, scores, masked_score)
            new_max = jnp.maximum(running_max, jnp.max(scores, axis=3))
            weights = jnp.where(allowed, jnp.exp(scores - new_max[..., None]), 0.0)
            factor = jnp.exp(running_max - new_max)
            new_sum = running_sum * factor + jnp.sum(weights, axis=3)
            partial_out = jnp.einsum(
                "hgqk,khd->qhgd",
                weights.astype(jnp.bfloat16),
                value_block,
                preferred_element_type=jnp.float32,
            )
            new_out = running_out * jnp.transpose(factor, (2, 0, 1))[..., None] + partial_out
            return (new_max, new_sum, new_out)

        def keep_state(inner_state):
            return inner_state

        return lax.cond(jnp.min(key_pos) <= query_top, update, keep_state, state)

    initial = (
        jnp.full((kv_heads, head_group, tok_rows), masked_score, jnp.float32),
        jnp.zeros((kv_heads, head_group, tok_rows), jnp.float32),
        jnp.zeros((tok_rows, kv_heads, head_group, HEAD_SIZE), jnp.float32),
    )
    running_max, running_sum, running_out = lax.fori_loop(
        0, total_rows // block_rows, absorb_block, initial
    )
    attended = (
        (running_out / jnp.transpose(running_sum, (2, 0, 1))[..., None])
        .reshape(tok_rows, width_q)
        .astype(jnp.bfloat16)
    )
    ids_flat = route_ids[:, 0]
    chosen = (ids_flat[:, None] == jnp.arange(EXPERTS, dtype=jnp.int32)[None, :]).astype(jnp.int32)
    ranking = jnp.sum((jnp.cumsum(chosen, axis=0) - chosen) * chosen, axis=1)
    slot_of = ids_flat * CAP + ranking
    selector = (jnp.arange(EXPERTS * CAP, dtype=jnp.int32)[:, None] == slot_of[None, :]).astype(
        jnp.bfloat16
    )
    host_count = ctx_count // EXPERTS
    feature_width = hidden.shape[1]
    packed = jnp.dot(selector, hidden, preferred_element_type=jnp.float32).astype(jnp.bfloat16)
    packed = jnp.broadcast_to(
        packed.reshape(EXPERTS, 1, CAP, feature_width), (EXPERTS, host_count, CAP, feature_width)
    ).reshape(ctx_count, CAP, feature_width)
    arrived = lax.all_to_all(packed, "ctx", split_axis=0, concat_axis=0, tiled=True)
    arrived = lax.all_gather(arrived, "tp", axis=2, tiled=True)
    slot_count = arrived.shape[1]
    flat_rows = arrived.reshape(-1, arrived.shape[2])
    gate_val = jnp.dot(flat_rows, w_gate[0], preferred_element_type=jnp.float32)
    up_val = jnp.dot(flat_rows, w_up[0], preferred_element_type=jnp.float32)
    inner = (jax.nn.silu(gate_val) * up_val).astype(jnp.bfloat16)
    pair_inner = lax.all_gather(inner, "tp", axis=1, tiled=True)
    partial_out = jnp.dot(pair_inner, w_down[0], preferred_element_type=jnp.float32).astype(
        jnp.bfloat16
    )
    partial_out = partial_out.reshape(ctx_count, slot_count, partial_out.shape[1])
    returned = lax.all_to_all(partial_out, "ctx", split_axis=0, concat_axis=0, tiled=True)
    out_width = returned.shape[2]
    summed = returned.reshape(EXPERTS, host_count, CAP, out_width).astype(jnp.float32).sum(axis=1)
    summed = summed.reshape(EXPERTS * CAP, out_width)
    mixed = (summed[slot_of] * route_gain[:, None]).astype(jnp.bfloat16)
    return (attended, mixed)


def solution(mesh):
    in_specs = (
        P("ctx", "tp"),
        P("ctx", "tp"),
        P("ctx", "tp"),
        P("ctx", "tp"),
        P("ctx", None),
        P("ctx"),
        P("ctx", None, "tp"),
        P("ctx", None, "tp"),
        P("ctx", None, "tp"),
    )
    out_specs = (P("ctx", "tp"), P("ctx", "tp"))
    return jax.shard_map(body, mesh=mesh, in_specs=in_specs, out_specs=out_specs, check_vma=False)
```

profile of v0, /device:TPU:0, one launch (start us, length us, event | category | flops | bytes accessed | tf_op | source)
XLA Modules:
  0.0 152.1 jit_solution(1355597205857069275)
XLA Ops:
  0.7 0.8 fusion.35
  1.5 0.8 select_reduce_fusion
  2.4 0.7 multiply_add_fusion.1
  3.3 1.0 reshape_reshape.3
  4.3 8.3 %all-to-all-start = ((bf16[16,6,2560]{2,1,0:T(8,128)(2,1)}), bf16[16,6,2560]{2,1,0:T(8,128)(2,1)S(1)}, u32[]{:S(2)}, u32[]{:S(2)}) async-start(bf16[16,6,2560]{2,1,0:T(8,128)(2,1)} %reshape_reshape.3), calls=%async_computation | async-start | bytes 1310720 | tf_op jit(solution)/shard_map/all_to_all | solution.py:105
  12.7 0.6 fusion.48
  13.3 0.6 fusion.46
  15.3 45.2 %all_gather.12 = bf16[1024,256]{1,0:T(8,128)(2,1)S(1)} all-gather(bf16[64,256]{1,0:T(8,128)(2,1)S(1)} %copy-done.4), channel_id=1, replica_groups=mesh['ctx'=16,'tp'=2] {'ctx'}, dimensions={0}, use_global_device_ids=true | all-gather | bytes 557056 | tf_op jit(solution)/shard_map/all_gather | solution.py:34
  60.5 2.7 %all_gather.14 = bf16[16,6,5120]{2,1,0:T(8,128)(2,1)S(1)} all-gather(bf16[16,6,2560]{2,1,0:T(8,128)(2,1)S(1)} %all-to-all-done), channel_id=1, replica_groups=mesh['ctx'=16,'tp'=2] {'tp'}, dimensions={2}, use_global_device_ids=true | all-gather | bytes 1474560 | tf_op jit(solution)/shard_map/all_gather | solution.py:106
  63.7 8.9 %fusion.24 = f32[96,2048]{1,0:T(8,128)S(1)} fusion(bf16[96,5120]{1,0:T(8,128)(2,1)S(1)} %reshape.55, bf16[1,5120,2048]{2,1,0:T(8,128)(2,1)} %param.17), kind=kOutput, calls=%fused_computation.26 | convolution fusion | flops 2013265920 | bytes 22740992 | tf_op jit(solution)/shard_map/dot_general | solution.py:109
  72.6 11.1 %fusion.32 = bf16[96,2048]{1,0:T(8,128)(2,1)S(1)} fusion(bf16[96,5120]{1,0:T(8,128)(2,1)S(1)} %reshape.55, bf16[1,5120,2048]{2,1,0:T(8,128)(2,1)} %param.18, f32[96,2048]{1,0:T(8,128)S(1)} %fusion.24), kind=kOutput, calls=%fused_computation.31 | convolution fusion | flops 2014445568 | bytes 23134208 | tf_op jit(solution)/shard_map/dot_general | solution.py:110
  83.7 2.4 %all_gather.15 = bf16[96,4096]{1,0:T(8,128)(2,1)S(1)} all-gather(bf16[96,2048]{1,0:T(8,128)(2,1)S(1)} %fusion.32), channel_id=1, replica_groups=mesh['ctx'=16,'tp'=2] {'tp'}, dimensions={1}, use_global_device_ids=true | all-gather | bytes 1179648 | tf_op jit(solution)/shard_map/all_gather | solution.py:112
  86.2 3.4 %fusion.26 = bf16[96,2560]{1,0:T(8,128)(2,1)S(1)} fusion(bf16[96,4096]{1,0:T(8,128)(2,1)S(1)} %all_gather.15, bf16[1,4096,2560]{2,1,0:T(8,128)(2,1)S(1)} %bitcast.52), kind=kOutput, calls=%fused_computation.28 | convolution fusion | flops 2013511680 | bytes 22249472 | tf_op jit(solution)/shard_map/dot_general | solution.py:113
  89.6 1.0 reshape.56
  90.6 3.6 %all-to-all-start.1 = ((bf16[16,6,2560]{2,1,0:T(8,128)(2,1)}), bf16[16,6,2560]{2,1,0:T(8,128)(2,1)S(1)}, u32[]{:S(2)}, u32[]{:S(2)}) async-start(bf16[16,6,2560]{2,1,0:T(8,128)(2,1)} %reshape.56), calls=%async_computation.1 | async-start | bytes 1310720 | tf_op jit(solution)/shard_map/all_to_all | solution.py:117
  94.2 48.7 %all_gather.13 = bf16[1024,256]{1,0:T(8,128)(2,1)S(1)} all-gather(bf16[64,256]{1,0:T(8,128)(2,1)S(1)} %copy-done.5), channel_id=1, replica_groups=mesh['ctx'=16,'tp'=2] {'ctx'}, dimensions={0}, use_global_device_ids=true | all-gather | bytes 557056 | tf_op jit(solution)/shard_map/all_gather | solution.py:35
  142.9 6.3 %conditional.1 = ((f32[2,5,64]{2,1,0:T(8,128)S(1)}, f32[64,2,5,128]{3,0,2,1:T(8,128)S(1)})) conditional(s32[]{:T(128)} %convert_element_type.33, (f32[2,5,64]{2,1,0:T(8,128)S(1)}, f32[64,2,5,128]{3,0,2,1:T(8,128)S(1)}) %tuple.25, (s32[64]{0:T(128)S(1)}, s32[1024]{0:T(1024)S(1)}, bf16[1024,256]{1,0:T(8,128)(2,1)S(1)}, bf16[64,1280]{1,0:T(8,128)(2,1)S(1)}, ...), branch_computations={%region_2.3_spmd, %region_3.6_spmd} | conditional | flops 344295296 | bytes 22939956 | solution.py:77
  143.3 0.7 fusion
  144.0 1.5 copy-done.2
  145.5 0.8 fusion.2
  146.5 2.6 %fusion.9 = f32[64,2,5,128]{3,0,2,1:T(8,128)S(1)} fusion(f32[2,1024,64,5]{1,2,3,0:T(8,128)} %copy-done.2, f32[2,5,64]{2,1,0:T(8,128)S(1)} %broadcast_maximum_fusion, pred[64,1024]{1,0:T(8,128)(4,1)S(1)} %broadcast_compare_fusion, bf16[1024,2,128,1]{2,1,0,3:T(2,128)(2,1)S(1)} %bitcast.53, f32[64,2,5,128]{3,0,2,1:T(8,128)S(1)} %get-tuple-element.89, ...), kind=kOutput, calls=%fused_computation.9 | convolution fusion | flops 171212800 | bytes 3871744 | tf_op jit(solution)/shard_map/while/body/eval_jaxpr/cond/branch_1_fun/hgqk,khd->qhgd/dot_general | solution.py:65
  149.4 0.9 convert_element_type.35
  150.5 0.8 gather_fusion
  151.3 0.8 multiply_convert_fusion
  (46 shorter events, 1.8 us)
Async XLA Ops:
  0.6 2.4 %copy-start = (bf16[64,2560]{1,0:T(8,128)(2,1)S(1)}, bf16[64,2560]{1,0:T(8,128)(2,1)}, u32[]{:S(2)}) copy-start(bf16[64,2560]{1,0:T(8,128)(2,1)} %param.14) | copy-start | bytes 983044
  0.6 14.6 %copy-start.4 = (bf16[64,256]{1,0:T(8,128)(2,1)S(1)}, bf16[64,256]{1,0:T(8,128)(2,1)}, u32[]{:S(2)}) copy-start(bf16[64,256]{1,0:T(8,128)(2,1)} %param.12) | copy-start | bytes 98308
  4.3 56.2 %all-to-all-start = ((bf16[16,6,2560]{2,1,0:T(8,128)(2,1)}), bf16[16,6,2560]{2,1,0:T(8,128)(2,1)S(1)}, u32[]{:S(2)}, u32[]{:S(2)}) async-start(bf16[16,6,2560]{2,1,0:T(8,128)(2,1)} %reshape_reshape.3), calls=%async_computation | async-start | bytes 1310720 | tf_op jit(solution)/shard_map/all_to_all | solution.py:105
  63.6 22.5 %slice-start = ((s8[20971520]{0:T(1024)(128)(4,1)}), s8[4194304]{0:T(1024)(128)(4,1)S(1)}, s32[]{:S(2)}) async-start(s8[20971520]{0:T(1024)(128)(4,1)} %bitcast.51), calls=%async_computation.2 | async-start | bytes 8388608
  63.6 22.5 %slice-start.1 = ((s8[20971520]{0:T(1024)(128)(4,1)}), s8[4194304]{0:T(1024)(128)(4,1)S(1)}, s32[]{:S(2)}) async-start(s8[20971520]{0:T(1024)(128)(4,1)} %bitcast.51), calls=%async_computation.3 | async-start | bytes 8388608
  63.7 22.5 %slice-start.2 = ((s8[20971520]{0:T(1024)(128)(4,1)}), s8[4194304]{0:T(1024)(128)(4,1)S(1)}, s32[]{:S(2)}) async-start(s8[20971520]{0:T(1024)(128)(4,1)} %bitcast.51), calls=%async_computation.4 | async-start | bytes 8388608
  72.6 13.5 %slice-start.3 = ((s8[20971520]{0:T(1024)(128)(4,1)}), s8[4194304]{0:T(1024)(128)(4,1)S(1)}, s32[]{:S(2)}) async-start(s8[20971520]{0:T(1024)(128)(4,1)} %bitcast.51), calls=%async_computation.5 | async-start | bytes 8388608
  72.6 13.5 %slice-start.4 = ((s8[20971520]{0:T(1024)(128)(4,1)}), s8[4194304]{0:T(1024)(128)(4,1)S(1)}, s32[]{:S(2)}) async-start(s8[20971520]{0:T(1024)(128)(4,1)} %bitcast.51), calls=%async_computation.6 | async-start | bytes 8388608
  86.2 8.1 %copy-start.5 = (bf16[64,256]{1,0:T(8,128)(2,1)S(1)}, bf16[64,256]{1,0:T(8,128)(2,1)}, u32[]{:S(2)}) copy-start(bf16[64,256]{1,0:T(8,128)(2,1)} %param.13) | copy-start | bytes 98308
  89.6 53.3 %copy-start.3 = (bf16[64,1280]{1,0:T(8,128)(2,1)S(1)}, bf16[64,1280]{1,0:T(8,128)(2,1)}, u32[]{:S(2)}) copy-start(bf16[64,1280]{1,0:T(8,128)(2,1)} %param.11) | copy-start | bytes 491524
  90.6 59.7 %all-to-all-start.1 = ((bf16[16,6,2560]{2,1,0:T(8,128)(2,1)}), bf16[16,6,2560]{2,1,0:T(8,128)(2,1)S(1)}, u32[]{:S(2)}, u32[]{:S(2)}) async-start(bf16[16,6,2560]{2,1,0:T(8,128)(2,1)} %reshape.56), calls=%async_computation.1 | async-start | bytes 1310720 | tf_op jit(solution)/shard_map/all_to_all | solution.py:117
  142.9 7.4 %copy-start.6 = (s32[64,1]{0,1:T(1,128)S(1)}, s32[64,1]{0,1:T(1,128)}, u32[]{:S(2)}) copy-start(s32[64,1]{0,1:T(1,128)} %param.15) | copy-start | bytes 772
  144.0 1.5 copy-start.2
  150.3 1.8 %copy-start.1 = (bf16[64,2560]{1,0:T(8,128)(2,1)S(1)}, bf16[64,2560]{1,0:T(8,128)(2,1)}, u32[]{:S(2)}) copy-start(bf16[64,2560]{1,0:T(8,128)(2,1)} %param.14) | copy-start | bytes 983044
  150.5 0.8 copy-start.7
where the time goes:
time: 153 us; the launch traced here: 152 us
  blocking collectives  99 us (65%)
  matrix products  27 us (18%)
  starting transfers between devices  11.9 us (8%)
  local copies, waits for them, and re-layouts  6.33 us (4%)
  other arithmetic  5.61 us (4%)
  between operations  2.2 us (1%)
    all_gather x1, blocking collectives, body(): lax.all_gather(value_use, 'ctx', axis=0, tiled=True)  48.7 us
    all_gather x1, blocking collectives, body(): lax.all_gather(key_use, 'ctx', axis=0, tiled=True)  45.2 us
    dot_general x1, matrix products, body(): up_val = jnp.dot(flat_rows, w_up[0], preferred_element_type=jnp.float32)  11.1 us
    dot_general x1, matrix products, body(): gate_val = jnp.dot(flat_rows, w_gate[0], preferred_element_type=jnp.float32)  8.92 us
    all_to_all x1, starting transfers between devices, body(): lax.all_to_all(packed, 'ctx', split_axis=0, concat_axis=0, tiled=True)  8.34 us
    all_to_all x1, starting transfers between devices, body(): lax.all_to_all(partial_out, 'ctx', split_axis=0, concat_axis=0, tiled=True)  3.59 us
    dot_general x1, matrix products, body(): jnp.dot(pair_inner, w_down[0], preferred_element_type=jnp.float32)  3.41 us
  transfers between devices with their start and end apart: 2, of which 0 were waited for; matrix products, arithmetic and copies ran while one was open for 5% of the time, Pallas kernels for 0%

commit v1 on v0

--- a/solution.py
+++ b/solution.py
@@ -8,6 +8,18 @@
 EXPERTS = 16
 CAP = 6
 masked_score = -1e30
+
+
+def doubled_up(value, axis, dim):
+    ways, here, step = (lax.axis_size(axis), lax.axis_index(axis), value.shape[dim])
+    line, have = (value, 1)
+    while have < ways:
+        line = jnp.concatenate(
+            [line, lax.ppermute(line, axis, [(d, (d - have) % ways) for d in range(ways)])],
+            axis=dim,
+        )
+        have = 2 * have
+    return jnp.roll(line, here * step, axis=dim)
 
 
 def body(
@@ -32,7 +44,7 @@
     score_scale = HEAD_SIZE ** (-0.5)
     key_whole, value_whole = (
         lax.all_gather(key_use, "ctx", axis=0, tiled=True),
-        lax.all_gather(value_use, "ctx", axis=0, tiled=True),
+        doubled_up(value_use, "ctx", 0),
     )
     total_rows = key_whole.shape[0]
     block_rows = math.gcd(total_rows, 1024)

time: 153 us -> 139 us (0.908)
  blocking collectives: 99 us -> 53.8 us
  starting transfers between devices: 11.9 us -> 30 us
  waiting for transfers between devices: 0.01 us -> 11.3 us
  local copies, waits for them, and re-layouts: 6.33 us -> 8.18 us
    all_gather x1 -> x0, blocking collectives: 48.7 us -> none  [body(): lax.all_gather(value_use, 'ctx', axis=0, tiled=True)]
    ppermute x0 -> x4, starting transfers between devices: none -> 12.1 us  [doubled_up(): lax.ppermute(line, axis, [(d, (d - have) % ways) for d in range(ways)])]
    ppermute x0 -> x4, waiting for transfers between devices: none -> 11.3 us  [doubled_up(): lax.ppermute(line, axis, [(d, (d - have) % ways) for d in range(ways)])]
    all_to_all x1, starting transfers between devices: 3.59 us -> 9.59 us  [body(): lax.all_to_all(partial_out, 'ctx', split_axis=0, concat_axis=0, tiled=True)]
    all_gather x1, blocking collectives: 45.2 us -> 48.7 us  [body(): lax.all_gather(key_use, 'ctx', axis=0, tiled=True)]
    concatenate x0 -> x1, local copies, waits for them, and re-layouts: none -> 1.63 us  [doubled_up(): return jnp.roll(line, here * step, axis=dim)]
  transfers between devices with their start and end apart: 2 -> 6, of which waited for: 0 -> 2; matrix products, arithmetic and copies ran while one was open for 5% -> 25% of each run, Pallas kernels for 0% -> 0%
where the time goes in v1:
time: 139 us
  blocking collectives  53.8 us (39%)
  starting transfers between devices  30 us (22%)
  matrix products  27 us (19%)
  waiting for transfers between devices  11.3 us (8%)
  local copies, waits for them, and re-layouts  8.18 us (6%)
  other arithmetic  5.93 us (4%)
  between operations  2.16 us (2%)
    all_gather x1, blocking collectives, body(): lax.all_gather(key_use, 'ctx', axis=0, tiled=True)  48.7 us
    ppermute x4, starting transfers between devices, doubled_up(): lax.ppermute(line, axis, [(d, (d - have) % ways) for d in range(ways)])  12.1 us
    ppermute x4, waiting for transfers between devices, doubled_up(): lax.ppermute(line, axis, [(d, (d - have) % ways) for d in range(ways)])  11.3 us
    dot_general x1, matrix products, body(): up_val = jnp.dot(flat_rows, w_up[0], preferred_element_type=jnp.float32)  11.1 us
    all_to_all x1, starting transfers between devices, body(): lax.all_to_all(partial_out, 'ctx', split_axis=0, concat_axis=0, tiled=True)  9.59 us
    dot_general x1, matrix products, body(): gate_val = jnp.dot(flat_rows, w_gate[0], preferred_element_type=jnp.float32)  8.92 us
    all_to_all x1, starting transfers between devices, body(): lax.all_to_all(packed, 'ctx', split_axis=0, concat_axis=0, tiled=True)  8.34 us
    dot_general x1, matrix products, body(): jnp.dot(pair_inner, w_down[0], preferred_element_type=jnp.float32)  3.41 us
  transfers between devices with their start and end apart: 6, of which 2 were waited for; matrix products, arithmetic and copies ran while one was open for 25% of the time, Pallas kernels for 0%

profile of v1, /device:TPU:0, one launch (start us, length us, event | category | flops | bytes accessed | tf_op | source)
XLA Modules:
  0.0 138.7 jit_solution(10570017225256986352)
XLA Ops:
  1.5 0.8 select_reduce_fusion
  3.3 1.0 reshape_reshape.3
  4.3 8.3 %all-to-all-start = ((bf16[16,6,2560]{2,1,0:T(8,128)(2,1)}), bf16[16,6,2560]{2,1,0:T(8,128)(2,1)S(1)}, u32[]{:S(2)}, u32[]{:S(2)}) async-start(bf16[16,6,2560]{2,1,0:T(8,128)(2,1)} %reshape_reshape.3), calls=%async_computation | async-start | bytes 1310720 | tf_op jit(solution)/shard_map/all_to_all | solution.py:117
  12.8 5.6 %collective-permute-start = (bf16[64,256]{0,1:T(8,128)(2,1)S(1)}, bf16[64,256]{0,1:T(8,128)(2,1)S(1)}, u32[]{:S(2)}, u32[]{:S(2)}) collective-permute-start(bf16[64,256]{0,1:T(8,128)(2,1)S(1)} %copy.23), channel_id=1, source_target_pairs={{0,30},{2,0},{4,2},{6,4},{8,6},{10,8},{12,10},{14,12},{16,14},{18,... | collective-permute-start | bytes 98312 | tf_op jit(solution)/shard_map/ppermute | solution.py:18
  18.4 6.8 %collective-permute-done = bf16[64,256]{0,1:T(8,128)(2,1)S(1)} collective-permute-done((bf16[64,256]{0,1:T(8,128)(2,1)S(1)}, bf16[64,256]{0,1:T(8,128)(2,1)S(1)}, u32[]{:S(2)}, u32[]{:S(2)}) %collective-permute-start) | collective-permute-done | bytes 32800 | tf_op jit(solution)/shard_map/ppermute | solution.py:18
  25.3 4.6 %collective-permute-done.1 = bf16[128,256]{0,1:T(8,128)(2,1)S(1)} collective-permute-done((bf16[128,256]{0,1:T(8,128)(2,1)S(1)}, bf16[128,256]{0,1:T(8,128)(2,1)S(1)}, u32[]{:S(2)}, u32[]{:S(2)}) %collective-permute-start.1) | collective-permute-done | bytes 65568 | tf_op jit(solution)/shard_map/ppermute | solution.py:18
  30.0 3.5 %collective-permute-start.2 = (bf16[256,256]{0,1:T(8,128)(2,1)S(1)}, bf16[256,256]{0,1:T(8,128)(2,1)S(1)}, u32[]{:S(2)}, u32[]{:S(2)}) collective-permute-start(bf16[256,256]{0,1:T(8,128)(2,1)S(1)} %pad_maximum_fusion.1), channel_id=1, source_target_pairs={{0,24},{2,26},{4,28},{6,30},{8,0},{10,2},{12,4},{14,6},{16,8},{18,... | collective-permute-start | bytes 393224 | tf_op jit(solution)/shard_map/ppermute | solution.py:18
  33.6 2.7 %all_gather.10 = bf16[16,6,5120]{2,1,0:T(8,128)(2,1)S(1)} all-gather(bf16[16,6,2560]{2,1,0:T(8,128)(2,1)S(1)} %all-to-all-done), channel_id=1, replica_groups=mesh['ctx'=16,'tp'=2] {'tp'}, dimensions={2}, use_global_device_ids=true | all-gather | bytes 1474560 | tf_op jit(solution)/shard_map/all_gather | solution.py:118
  36.7 8.9 %fusion.23 = f32[96,2048]{1,0:T(8,128)S(1)} fusion(bf16[96,5120]{1,0:T(8,128)(2,1)S(1)} %reshape.61, bf16[1,5120,2048]{2,1,0:T(8,128)(2,1)} %param.17), kind=kOutput, calls=%fused_computation.26 | convolution fusion | flops 2013265920 | bytes 22740992 | tf_op jit(solution)/shard_map/dot_general | solution.py:121
  45.6 11.1 %fusion.31 = bf16[96,2048]{1,0:T(8,128)(2,1)S(1)} fusion(bf16[96,5120]{1,0:T(8,128)(2,1)S(1)} %reshape.61, bf16[1,5120,2048]{2,1,0:T(8,128)(2,1)} %param.18, f32[96,2048]{1,0:T(8,128)S(1)} %fusion.23), kind=kOutput, calls=%fused_computation.31 | convolution fusion | flops 2014445568 | bytes 23134208 | tf_op jit(solution)/shard_map/dot_general | solution.py:122
  56.8 2.4 %all_gather.11 = bf16[96,4096]{1,0:T(8,128)(2,1)S(1)} all-gather(bf16[96,2048]{1,0:T(8,128)(2,1)S(1)} %fusion.31), channel_id=1, replica_groups=mesh['ctx'=16,'tp'=2] {'tp'}, dimensions={1}, use_global_device_ids=true | all-gather | bytes 1179648 | tf_op jit(solution)/shard_map/all_gather | solution.py:124
  59.2 3.4 %fusion.25 = bf16[96,2560]{1,0:T(8,128)(2,1)S(1)} fusion(bf16[96,4096]{1,0:T(8,128)(2,1)S(1)} %all_gather.11, bf16[1,4096,2560]{2,1,0:T(8,128)(2,1)S(1)} %bitcast.57), kind=kOutput, calls=%fused_computation.28 | convolution fusion | flops 2013511680 | bytes 22249472 | tf_op jit(solution)/shard_map/dot_general | solution.py:125
  62.6 1.0 reshape.62
  63.6 9.6 %all-to-all-start.1 = ((bf16[16,6,2560]{2,1,0:T(8,128)(2,1)}), bf16[16,6,2560]{2,1,0:T(8,128)(2,1)S(1)}, u32[]{:S(2)}, u32[]{:S(2)}) async-start(bf16[16,6,2560]{2,1,0:T(8,128)(2,1)} %reshape.62), calls=%async_computation.1 | async-start | bytes 1310720 | tf_op jit(solution)/shard_map/all_to_all | solution.py:129
  73.4 2.9 %collective-permute-start.3 = (bf16[512,256]{0,1:T(8,128)(2,1)S(1)}, bf16[512,256]{0,1:T(8,128)(2,1)S(1)}, u32[]{:S(2)}, u32[]{:S(2)}) collective-permute-start(bf16[512,256]{0,1:T(8,128)(2,1)S(1)} %pad_maximum_fusion), channel_id=1, source_target_pairs={{0,16},{2,18},{4,20},{6,22},{8,24},{10,26},{12,28},{14,30},{16,0},... | collective-permute-start | bytes 786440 | tf_op jit(solution)/shard_map/ppermute | solution.py:18
  78.8 48.7 %all_gather.9 = bf16[1024,256]{1,0:T(8,128)(2,1)S(1)} all-gather(bf16[64,256]{1,0:T(8,128)(2,1)S(1)} %copy-done.5), channel_id=1, replica_groups=mesh['ctx'=16,'tp'=2] {'ctx'}, dimensions={0}, use_global_device_ids=true | all-gather | bytes 557056 | tf_op jit(solution)/shard_map/all_gather | solution.py:46
  127.5 1.6 %concatenate.21 = bf16[2048,256]{0,1:T(8,128)(2,1)S(1)} concatenate(bf16[64,256]{0,1:T(8,128)(2,1)S(1)} %copy.23, bf16[64,256]{0,1:T(8,128)(2,1)S(1)} %collective-permute-done, bf16[128,256]{0,1:T(8,128)(2,1)S(1)} %collective-permute-done.1, bf16[256,256]{0,1:T(8,128)(2,1)S(1)} %collective-permute-done.2, bf16[512,256]{0,1:T(8,128)(2,1)S(1)} %collective-permute-done.3, ...), dimensions={0} | concatenate | bytes 2097152 | tf_op jit(solution)/shard_map/jit(_roll_dynamic)/concatenate | solution.py:22
  129.2 6.6 %conditional.1 = ((f32[2,5,64]{2,1,0:T(8,128)S(1)}, f32[64,2,5,128]{3,0,2,1:T(8,128)S(1)})) conditional(s32[]{:T(128)} %convert_element_type.35, (f32[2,5,64]{2,1,0:T(8,128)S(1)}, f32[64,2,5,128]{3,0,2,1:T(8,128)S(1)}) %tuple.39, (s32[64]{0:T(128)S(1)}, s32[1024]{0:T(1024)S(1)}, bf16[1024,256]{1,0:T(8,128)(2,1)S(1)}, ...), branch_computations={%region_2.3_spmd, %region_3.6_spmd.clone} | conditional | flops 344295296 | bytes 22940116 | solution.py:89
  130.5 1.5 %copy-done.2 = f32[2,1024,64,5]{1,2,3,0:T(8,128)} copy-done((f32[2,1024,64,5]{1,2,3,0:T(8,128)}, f32[2,1024,64,5]{1,2,3,0:T(8,128)S(1)}, u32[]{:S(2)}) %copy-start.2) | copy-done | bytes 2621464 | tf_op jit(solution)/shard_map/while/body/eval_jaxpr/cond
  132.0 0.8 fusion.2
  133.1 2.6 %fusion.9 = f32[64,2,5,128]{3,0,2,1:T(8,128)S(1)} fusion(bf16[1024,2,128,1]{0,2,3,1:T(8,128)(2,1)S(1)} %bitcast.59, f32[2,1024,64,5]{1,2,3,0:T(8,128)} %copy-done.2, f32[2,5,64]{2,1,0:T(8,128)S(1)} %broadcast_maximum_fusion, pred[64,1024]{1,0:T(8,128)(4,1)S(1)} %broadcast_compare_fusion, f32[64,2,5,128]{3,0,2,1:T(8,128)S(1)} %get-tuple-element.200, ...), kind=kOutput, calls=%fused_computation.9 | convolution fusion | flops 171212800 | bytes 3871744 | tf_op jit(solution)/shard_map/while/body/eval_jaxpr/cond/branch_1_fun/hgqk,khd->qhgd/dot_general | solution.py:77
  136.0 0.9 convert_element_type.37
  137.0 0.8 gather_fusion
  137.9 0.8 multiply_convert_fusion
  (58 shorter events, 5.8 us)
Async XLA Ops:
  0.6 2.4 %copy-start = (bf16[64,2560]{1,0:T(8,128)(2,1)S(1)}, bf16[64,2560]{1,0:T(8,128)(2,1)}, u32[]{:S(2)}) copy-start(bf16[64,2560]{1,0:T(8,128)(2,1)} %param.14) | copy-start | bytes 983044
  0.6 24.7 %copy-start.6 = (s32[64,1]{0,1:T(1,128)S(1)}, s32[64,1]{0,1:T(1,128)}, u32[]{:S(2)}) copy-start(s32[64,1]{0,1:T(1,128)} %param.15) | copy-start | bytes 772
  0.7 12.0 %copy-start.4 = (bf16[64,256]{1,0:T(8,128)(2,1)S(1)}, bf16[64,256]{1,0:T(8,128)(2,1)}, u32[]{:S(2)}) copy-start(bf16[64,256]{1,0:T(8,128)(2,1)} %param.13) | copy-start | bytes 98308
  4.3 29.2 %all-to-all-start = ((bf16[16,6,2560]{2,1,0:T(8,128)(2,1)}), bf16[16,6,2560]{2,1,0:T(8,128)(2,1)S(1)}, u32[]{:S(2)}, u32[]{:S(2)}) async-start(bf16[16,6,2560]{2,1,0:T(8,128)(2,1)} %reshape_reshape.3), calls=%async_computation | async-start | bytes 1310720 | tf_op jit(solution)/shard_map/all_to_all | solution.py:117
  12.8 12.3 %collective-permute-start = (bf16[64,256]{0,1:T(8,128)(2,1)S(1)}, bf16[64,256]{0,1:T(8,128)(2,1)S(1)}, u32[]{:S(2)}, u32[]{:S(2)}) collective-permute-start(bf16[64,256]{0,1:T(8,128)(2,1)S(1)} %copy.23), channel_id=1, source_target_pairs={{0,30},{2,0},{4,2},{6,4},{8,6},{10,8},{12,10},{14,12},{16,14},{18,... | collective-permute-start | bytes 98312 | tf_op jit(solution)/shard_map/ppermute | solution.py:18
  25.3 4.7 %collective-permute-start.1 = (bf16[128,256]{0,1:T(8,128)(2,1)S(1)}, bf16[128,256]{0,1:T(8,128)(2,1)S(1)}, u32[]{:S(2)}, u32[]{:S(2)}) collective-permute-start(bf16[128,256]{0,1:T(8,128)(2,1)S(1)} %pad_maximum_fusion.2), channel_id=1, source_target_pairs={{0,28},{2,30},{4,0},{6,2},{8,4},{10,6},{12,8},{14,10},{16,12},{18,... | collective-permute-start | bytes 196616 | tf_op jit(solution)/shard_map/ppermute | solution.py:18
  30.0 43.2 %collective-permute-start.2 = (bf16[256,256]{0,1:T(8,128)(2,1)S(1)}, bf16[256,256]{0,1:T(8,128)(2,1)S(1)}, u32[]{:S(2)}, u32[]{:S(2)}) collective-permute-start(bf16[256,256]{0,1:T(8,128)(2,1)S(1)} %pad_maximum_fusion.1), channel_id=1, source_target_pairs={{0,24},{2,26},{4,28},{6,30},{8,0},{10,2},{12,4},{14,6},{16,8},{18,... | collective-permute-start | bytes 393224 | tf_op jit(solution)/shard_map/ppermute | solution.py:18
  36.7 22.5 %slice-start = ((s8[20971520]{0:T(1024)(128)(4,1)}), s8[4194304]{0:T(1024)(128)(4,1)S(1)}, s32[]{:S(2)}) async-start(s8[20971520]{0:T(1024)(128)(4,1)} %bitcast.56), calls=%async_computation.2 | async-start | bytes 8388608
  36.7 22.5 %slice-start.1 = ((s8[20971520]{0:T(1024)(128)(4,1)}), s8[4194304]{0:T(1024)(128)(4,1)S(1)}, s32[]{:S(2)}) async-start(s8[20971520]{0:T(1024)(128)(4,1)} %bitcast.56), calls=%async_computation.3 | async-start | bytes 8388608
  36.7 22.5 %slice-start.2 = ((s8[20971520]{0:T(1024)(128)(4,1)}), s8[4194304]{0:T(1024)(128)(4,1)S(1)}, s32[]{:S(2)}) async-start(s8[20971520]{0:T(1024)(128)(4,1)} %bitcast.56), calls=%async_computation.4 | async-start | bytes 8388608
  45.6 13.5 %slice-start.3 = ((s8[20971520]{0:T(1024)(128)(4,1)}), s8[4194304]{0:T(1024)(128)(4,1)S(1)}, s32[]{:S(2)}) async-start(s8[20971520]{0:T(1024)(128)(4,1)} %bitcast.56), calls=%async_computation.5 | async-start | bytes 8388608
  45.6 13.5 %slice-start.4 = ((s8[20971520]{0:T(1024)(128)(4,1)}), s8[4194304]{0:T(1024)(128)(4,1)S(1)}, s32[]{:S(2)}) async-start(s8[20971520]{0:T(1024)(128)(4,1)} %bitcast.56), calls=%async_computation.6 | async-start | bytes 8388608
  62.6 16.2 %copy-start.5 = (bf16[64,256]{1,0:T(8,128)(2,1)S(1)}, bf16[64,256]{1,0:T(8,128)(2,1)}, u32[]{:S(2)}) copy-start(bf16[64,256]{1,0:T(8,128)(2,1)} %param.12) | copy-start | bytes 98308
  63.6 65.5 %copy-start.3 = (bf16[64,1280]{1,0:T(8,128)(2,1)S(1)}, bf16[64,1280]{1,0:T(8,128)(2,1)}, u32[]{:S(2)}) copy-start(bf16[64,1280]{1,0:T(8,128)(2,1)} %param.11) | copy-start | bytes 491524
  63.6 73.3 %all-to-all-start.1 = ((bf16[16,6,2560]{2,1,0:T(8,128)(2,1)}), bf16[16,6,2560]{2,1,0:T(8,128)(2,1)S(1)}, u32[]{:S(2)}, u32[]{:S(2)}) async-start(bf16[16,6,2560]{2,1,0:T(8,128)(2,1)} %reshape.62), calls=%async_computation.1 | async-start | bytes 1310720 | tf_op jit(solution)/shard_map/all_to_all | solution.py:129
  73.4 54.1 %collective-permute-start.3 = (bf16[512,256]{0,1:T(8,128)(2,1)S(1)}, bf16[512,256]{0,1:T(8,128)(2,1)S(1)}, u32[]{:S(2)}, u32[]{:S(2)}) collective-permute-start(bf16[512,256]{0,1:T(8,128)(2,1)S(1)} %pad_maximum_fusion), channel_id=1, source_target_pairs={{0,16},{2,18},{4,20},{6,22},{8,24},{10,26},{12,28},{14,30},{16,0},... | collective-permute-start | bytes 786440 | tf_op jit(solution)/shard_map/ppermute | solution.py:18
  130.5 1.5 %copy-start.2 = (f32[2,1024,64,5]{1,2,3,0:T(8,128)}, f32[2,1024,64,5]{1,2,3,0:T(8,128)S(1)}, u32[]{:S(2)}) copy-start(f32[2,1024,64,5]{1,2,3,0:T(8,128)S(1)} %get-tuple-element.223) | copy-start | bytes 7864324 | tf_op jit(solution)/shard_map/while/body/eval_jaxpr/cond
  136.9 1.8 %copy-start.1 = (bf16[64,2560]{1,0:T(8,128)(2,1)S(1)}, bf16[64,2560]{1,0:T(8,128)(2,1)}, u32[]{:S(2)}) copy-start(bf16[64,2560]{1,0:T(8,128)(2,1)} %param.14) | copy-start | bytes 983044
  137.0 0.8 copy-start.7
